TPU v7x, 32 devices: a whole 2x2x4 slice. The times are simulated.
32 devices in a mesh: blk: 8 (over y, x, core), walk: 4 (over z).
Axes of the slice: x: 2, y: 2, z: 4, core: 2. Of those that a mesh axis runs over, the one named last changes fastest.
Arguments:
- walker_m: bfloat16 [4, 8, 128, 128], P('walk', 'blk'), may hold values from -6 to 6
- vertex_times: int32 [4, 8, 128], P('walk', 'blk'), may hold values from 0 to 1023
- vertex_labels: int32 [4, 8, 128], P('walk', 'blk'), may hold values from 0 to 35
- freq_index: int32 [24], replicated, may hold values from -64 to 63
- q_index: int32 [8], P('blk'), may hold values from 0 to 35
Outputs:
- g4: float32 [8, 2, 864, 864], P('blk', None, 'walk')
Inputs may be any that keep to these rules, and one draw needn't show every extreme that they name: `q_index`: entry b is 6 qx + qy for the transfer momentum (qx, qy). `freq_index`: frequency f is pi (2 n + 1) / beta with n its entry. `vertex_times`: the time is entry * beta / 1024. `vertex_labels`: site s lies at row s // 6 and column s mod 6 of the 6×6 cluster.
All inputs are finite; a program needn't handle non-finite values.
Results may differ from a plain program's by a relative error of at most 0.0061.
Values may be sent and summed in bfloat16 or wider, within the bound.
A program may use at most 128 MiB of HBM per device.

v0:
```python
import math

import jax
import jax.numpy as jnp
from jax import lax
from jax.sharding import PartitionSpec as P

SIDE = 6
NF = 24
K = 864
V = 128
STEPS = 4
TGRID = 1024


TWO_PI = 2.0 * math.pi


def from_behind(value, axis, steps):
    count = lax.axis_size(axis)
    pairs = [(source, (source + steps) % count) for source in range(count)]
    return lax.ppermute(value, axis, pairs)


def phase_tables(time_points, labels, frequencies):
    modulus = 12 * TGRID
    momenta = jnp.arange(SIDE * SIDE, dtype=jnp.int32)
    momentum_across = momenta // SIDE
    momentum_down = momenta % SIDE
    site_across = labels // SIDE
    site_down = labels % SIDE
    freq_part = jnp.mod((2 * frequencies[:, None] + 1) * time_points[None, :] * 6, modulus)
    momentum_part = jnp.mod(
        2
        * TGRID
        * (
            momentum_across[:, None] * site_across[None, :]
            + momentum_down[:, None] * site_down[None, :]
        ),
        modulus,
    )
    phase = jnp.mod(freq_part[None, :, :] - momentum_part[:, None, :], modulus).reshape(
        SIDE * SIDE * NF, -1
    )
    angles = phase.astype(jnp.float32) * (TWO_PI / modulus)
    return (jnp.cos(angles).astype(jnp.bfloat16), jnp.sin(angles).astype(jnp.bfloat16))


def amplitudes(matrix, time_points, labels, frequencies):
    cos_table, sin_table = phase_tables(time_points, labels, frequencies)
    stacked = jnp.concatenate([cos_table, sin_table], axis=0)
    amplitude = jnp.dot(stacked, matrix, preferred_element_type=jnp.float32).astype(jnp.bfloat16)
    right_side = jnp.concatenate([cos_table, sin_table], axis=1)
    return (amplitude[:K], amplitude[K:], right_side)


def complex_left(real_part, imag_part):
    return jnp.concatenate(
        [
            jnp.concatenate([real_part, imag_part], axis=1),
            jnp.concatenate([imag_part, -real_part], axis=1),
        ],
        axis=0,
    )


def green_product(left_side, right_side, row_count, col_count):
    table = lax.dot_general(
        left_side, right_side, (((1,), (1,)), ((), ())), preferred_element_type=jnp.float32
    )
    return (table * (1.0 / V)).reshape(2, row_count, col_count)


def walker_term(matrix, time_points, labels, frequencies, shifted):
    real_part, imag_part, right_side = amplitudes(matrix, time_points, labels, frequencies)
    green_table = green_product(complex_left(real_part, imag_part), right_side, K, K)
    moved_left = complex_left(
        jnp.take(real_part, shifted, axis=0), jnp.take(imag_part, shifted, axis=0)
    )
    shifted_green = green_product(moved_left, jnp.take(right_side, shifted, axis=0), K, K)
    flipped = jnp.swapaxes(green_table, 1, 2)
    real_term = shifted_green[0] * flipped[0] - shifted_green[1] * flipped[1]
    imag_term = shifted_green[0] * flipped[1] + shifted_green[1] * flipped[0]
    return jnp.stack([real_term, imag_term])


def shifted_rows(transfer):
    row_index = jnp.arange(K, dtype=jnp.int32)
    momentum = row_index // NF
    offset = row_index % NF
    shift_across = (momentum // SIDE + transfer // SIDE) % SIDE
    shift_down = (momentum % SIDE + transfer % SIDE) % SIDE
    return (shift_across * SIDE + shift_down) * NF + offset


def settle(running, first_half):
    return (running, first_half)


def local(walker_m, vertex_times, vertex_labels, freq_index, q_index):
    group_count = lax.axis_size("walk")
    shifted = shifted_rows(q_index[0])
    first_half = None
    held = (walker_m, vertex_times, vertex_labels)
    running = jnp.zeros((2, K, K), jnp.float32)
    own_walker = (held[0][:, 0], held[1][:, 0], held[2][:, 0])

    def absorb(running, walker):
        running = running + walker_term(
            walker[0][0], walker[1][0], walker[2][0], freq_index, shifted
        )
        return running

    forward = own_walker
    backward = own_walker
    running = absorb(running, own_walker)
    running, first_half = settle(running, first_half)
    for number in range(1, STEPS):
        if number % 2 == 1:
            forward = from_behind((forward[0], forward[1], forward[2]), "blk", -1)
            walker = forward
        else:
            backward = from_behind((backward[0], backward[1], backward[2]), "blk", 1)
            walker = backward
        running = absorb(running, walker)
        running, first_half = settle(running, first_half)
    summed = lax.psum_scatter(running[None], "walk", scatter_dimension=2, tiled=True)
    return summed * (1.0 / (STEPS * group_count))


def solution(mesh):
    return jax.shard_map(
        local,
        mesh=mesh,
        in_specs=(
            P("walk", "blk", None, None),
            P("walk", "blk", None),
            P("walk", "blk", None),
            P(),
            P("blk"),
        ),
        out_specs=P("blk", None, "walk", None),
        check_vma=False,
    )
```

profile of v0, /device:TPU:0, one launch (start us, length us, event | category | flops | bytes accessed | tf_op | source)
XLA Modules:
  0.0 268.8 jit_solution(12565125343999568504)
XLA Ops:
  6.5 3.4 %collective-permute-start.1 = (s32[1,128]{1,0:T(1,128)}, s32[1,128]{1,0:T(1,128)S(1)}, u32[]{:S(2)}, u32[]{:S(2)}) collective-permute-start(s32[1,128]{1,0:T(1,128)} %bitcast.195), channel_id=1, source_target_pairs={{0,28},{4,0},{8,4},{12,8},{16,12},{20,16},{24,20},{28,24},{1,29},{... | collective-permute-start | bytes 1544 | tf_op jit(solution)/shard_map/ppermute | solution.py:22
  9.9 2.6 collective-permute-start
  12.5 2.6 collective-permute-start.2
  17.4 2.7 collective-permute-start.7
  31.3 3.7 %convolution_multiply_fusion.6 = f32[1728,864]{1,0:T(8,128)} fusion(bf16[864,128]{1,0:T(8,128)(2,1)S(1)} %get-tuple-element.39, bf16[864,128]{1,0:T(8,128)(2,1)S(1)} %get-tuple-element.40, bf16[864,128]{1,0:T(8,128)(2,1)S(1)} %get-tuple-element.38, bf16[864,128]{1,0:T(8,128)(2,1)S(1)} %get-tuple-element.42, bf16[864,128]{1,0:T(8,128)(2,1)S(1)} %get-tuple-element.41), kind=kOutput, calls=%fused_computation.21 | convolution fusion | flops 770328576 | bytes 7077888 | tf_op jit(solution)/shard_map/dot_general | solution.py:68
  35.1 3.0 %gather_fusion = bf16[864,128]{1,0:T(8,128)(2,1)} fusion(bf16[864,128]{1,0:T(8,128)(2,1)S(1)} %get-tuple-element.38, s32[1024]{0:T(1024)S(1)} %pad_clamp_fusion), kind=kCustom, calls=%fused_computation.clone | custom fusion | bytes 445824 | tf_op jit(solution)/shard_map/jit(_take)/gather | solution.py:78
  38.1 3.0 %gather_fusion.1 = bf16[864,128]{1,0:T(8,128)(2,1)} fusion(bf16[864,128]{1,0:T(8,128)(2,1)S(1)} %get-tuple-element.40, s32[1024]{0:T(1024)S(1)} %pad_clamp_fusion), kind=kCustom, calls=%fused_computation.2.clone | custom fusion | bytes 445824 | tf_op jit(solution)/shard_map/jit(_take)/gather | solution.py:78
  41.1 3.5 %gather_fusion.11 = bf16[864,256]{1,0:T(8,128)(2,1)S(1)} fusion(bf16[864,256]{1,0:T(8,128)(2,1)S(1)} %pad_maximum_fusion.3, s32[1024]{0:T(1024)S(1)} %pad_clamp_fusion), kind=kCustom, calls=%fused_computation.11.clone | custom fusion | bytes 888192 | tf_op jit(solution)/shard_map/jit(_take)/gather | solution.py:80
  44.6 3.9 %gather_fusion.8 = bf16[864,256]{1,0:T(8,128)(2,1)} fusion(bf16[864,256]{1,0:T(8,128)(2,1)S(1)} %pad_maximum_fusion.2, s32[1024]{0:T(1024)S(1)} %pad_clamp_fusion), kind=kCustom, calls=%fused_computation.10.clone | custom fusion | bytes 888192 | tf_op jit(solution)/shard_map/jit(_take)/gather | solution.py:80
  48.5 3.9 %gather_fusion.5 = bf16[864,256]{1,0:T(8,128)(2,1)} fusion(bf16[864,256]{1,0:T(8,128)(2,1)S(1)} %pad_maximum_fusion.1, s32[1024]{0:T(1024)S(1)} %pad_clamp_fusion), kind=kCustom, calls=%fused_computation.9.clone | custom fusion | bytes 888192 | tf_op jit(solution)/shard_map/jit(_take)/gather | solution.py:80
  52.5 3.9 %gather_fusion.2 = bf16[864,256]{1,0:T(8,128)(2,1)} fusion(bf16[864,256]{1,0:T(8,128)(2,1)S(1)} %pad_maximum_fusion, s32[1024]{0:T(1024)S(1)} %pad_clamp_fusion), kind=kCustom, calls=%fused_computation.1.clone | custom fusion | bytes 888192 | tf_op jit(solution)/shard_map/jit(_take)/gather | solution.py:80
  56.4 7.3 %copy.6 = f32[2,864,864]{1,2,0:T(8,128)} copy(f32[2,864,864]{2,1,0:T(8,128)} %bitcast.172) | data formatting | bytes 11943936 | tf_op jit(solution)/shard_map/reshape | solution.py:71
  65.9 3.7 %convolution_multiply_fusion.2 = f32[1728,864]{1,0:T(8,128)} fusion(bf16[864,128]{1,0:T(8,128)(2,1)S(1)} %get-tuple-element.29, bf16[864,128]{1,0:T(8,128)(2,1)S(1)} %get-tuple-element.30, bf16[864,128]{1,0:T(8,128)(2,1)S(1)} %get-tuple-element.28, bf16[864,128]{1,0:T(8,128)(2,1)S(1)} %get-tuple-element.32, bf16[864,128]{1,0:T(8,128)(2,1)S(1)} %get-tuple-element.31), kind=kOutput, calls=%fused_computation.17 | convolution fusion | flops 770328576 | bytes 7077888 | tf_op jit(solution)/shard_map/dot_general | solution.py:68
  69.6 2.7 %collective-permute-start.8 = (bf16[1,128,128]{2,1,0:T(8,128)(2,1)}, bf16[1,128,128]{2,1,0:T(8,128)(2,1)S(1)}, u32[]{:S(2)}, u32[]{:S(2)}) collective-permute-start(bf16[1,128,128]{2,1,0:T(8,128)(2,1)} %collective-permute-done.2), channel_id=1, source_target_pairs={{0,28},{4,0},{8,4},{12,8},{16,12},{20,16},{24,20},{28,24},{1,29},{... | collective-permute-start | bytes 98312 | tf_op jit(solution)/shard_map/ppermute | solution.py:22
  72.3 3.7 %convolution_multiply_fusion.4 = f32[1728,864]{1,0:T(8,128)} fusion(bf16[864,128]{1,0:T(8,128)(2,1)S(1)} %get-tuple-element.34, bf16[864,128]{1,0:T(8,128)(2,1)S(1)} %get-tuple-element.35, bf16[864,128]{1,0:T(8,128)(2,1)S(1)} %get-tuple-element.33, bf16[864,128]{1,0:T(8,128)(2,1)S(1)} %get-tuple-element.37, bf16[864,128]{1,0:T(8,128)(2,1)S(1)} %get-tuple-element.36), kind=kOutput, calls=%fused_computation.19 | convolution fusion | flops 770328576 | bytes 7077888 | tf_op jit(solution)/shard_map/dot_general | solution.py:68
  78.5 2.4 gather_fusion.4
  80.8 2.4 gather_fusion.6
  83.2 2.4 gather_fusion.7
  85.6 7.3 %copy.8 = f32[2,864,864]{1,2,0:T(8,128)} copy(f32[2,864,864]{2,1,0:T(8,128)} %bitcast.171) | data formatting | bytes 11943936 | tf_op jit(solution)/shard_map/reshape | solution.py:71
  92.9 7.3 %copy.7 = f32[2,864,864]{1,2,0:T(8,128)} copy(f32[2,864,864]{2,1,0:T(8,128)} %bitcast.173) | data formatting | bytes 11943936 | tf_op jit(solution)/shard_map/reshape | solution.py:71
  100.5 2.4 gather_fusion.9
  105.3 3.8 %convolution_multiply_fusion = f32[1728,864]{1,0:T(8,128)} fusion(bf16[864,128]{1,0:T(8,128)(2,1)S(1)} %get-tuple-element.24, bf16[864,128]{1,0:T(8,128)(2,1)S(1)} %get-tuple-element.25, bf16[864,128]{1,0:T(8,128)(2,1)S(1)} %get-tuple-element.23, bf16[864,128]{1,0:T(8,128)(2,1)S(1)} %get-tuple-element.27, bf16[864,128]{1,0:T(8,128)(2,1)S(1)} %get-tuple-element.26), kind=kOutput, calls=%fused_computation.15 | convolution fusion | flops 770328576 | bytes 7077888 | tf_op jit(solution)/shard_map/dot_general | solution.py:68
  109.1 7.4 %copy.9 = f32[2,864,864]{1,2,0:T(8,128)} copy(f32[2,864,864]{2,1,0:T(8,128)} %bitcast.174) | data formatting | bytes 11943936 | tf_op jit(solution)/shard_map/reshape | solution.py:71
  121.9 2.6 convolution_multiply_fusion.3
  124.8 3.2 %subtract_bitcast_fusion.1 = (f32[1,1,864,864]{3,2,1,0:T(8,128)}, f32[1,1,864,864]{3,2,1,0:T(8,128)}) fusion(f32[2,864,864]{2,1,0:T(8,128)S(1)} %bitcast.183, f32[1728,864]{1,0:T(8,128)S(1)} %convolution_multiply_fusion.3), kind=kLoop, calls=%fused_computation.34 | loop fusion | flops 4478976 | bytes 17915904 | tf_op jit(solution)/shard_map/stack | solution.py:84
  128.1 2.6 convolution_multiply_fusion.5
  131.3 3.2 %subtract_bitcast_fusion.2 = (f32[1,1,864,864]{3,2,1,0:T(8,128)}, f32[1,1,864,864]{3,2,1,0:T(8,128)}) fusion(f32[2,864,864]{2,1,0:T(8,128)S(1)} %bitcast.180, f32[1728,864]{1,0:T(8,128)S(1)} %convolution_multiply_fusion.5), kind=kLoop, calls=%fused_computation.36 | loop fusion | flops 4478976 | bytes 17915904 | tf_op jit(solution)/shard_map/stack | solution.py:84
  134.5 2.4 convolution_multiply_fusion.7
  137.6 3.3 %subtract_bitcast_fusion.3 = (f32[1,1,864,864]{3,2,1,0:T(8,128)}, f32[1,1,864,864]{3,2,1,0:T(8,128)}) fusion(f32[2,864,864]{2,1,0:T(8,128)S(1)} %bitcast.177, f32[1728,864]{1,0:T(8,128)S(1)} %convolution_multiply_fusion.7), kind=kLoop, calls=%fused_computation.38 | loop fusion | flops 4478976 | bytes 17915904 | tf_op jit(solution)/shard_map/stack | solution.py:84
  140.8 9.8 %fusion.1 = f32[1,2,864,864]{3,2,1,0:T(8,128)} fusion(f32[1,1,864,864]{3,2,1,0:T(8,128)} %get-tuple-element.22, f32[1,1,864,864]{3,2,1,0:T(8,128)} %get-tuple-element.21, f32[1,1,864,864]{3,2,1,0:T(8,128)} %get-tuple-element.20, f32[1,1,864,864]{3,2,1,0:T(8,128)} %get-tuple-element.19, f32[1,1,864,864]{3,2,1,0:T(8,128)} %get-tuple-element.18, ...), kind=kLoop, calls=%fused_computation.14 | loop fusion | flops 10450944 | bytes 29859840 | tf_op jit(solution)/shard_map/add | solution.py:109
  150.6 108.7 %reduce-scatter.2.cloned.1.call-done = f32[1,2,216,864]{3,2,1,0:T(8,128)} async-done(((f32[1,2,864,864]{3,2,1,0:T(8,128)}), f32[1,2,216,864]{3,2,1,0:T(8,128)}) %reduce-scatter.2.cloned.1.call-update) | async-done | bytes 1493008 | tf_op jit(solution)/shard_map/reduce_scatter | solution.py:127
  259.3 2.6 broadcast_multiply_fusion
  (80 shorter events, 26.9 us)
Async XLA Ops:
  6.5 252.8 %reduce-scatter.2.cloned.1.call-start = ((), (), s32[]{:S(2)}) async-start(), calls=%async_computation.1 | async-start | bytes 7741440 | tf_op jit(solution)/shard_map/reduce_scatter | solution.py:127
  6.5 10.8 %collective-permute-start.1 = (s32[1,128]{1,0:T(1,128)}, s32[1,128]{1,0:T(1,128)S(1)}, u32[]{:S(2)}, u32[]{:S(2)}) collective-permute-start(s32[1,128]{1,0:T(1,128)} %bitcast.195), channel_id=1, source_target_pairs={{0,28},{4,0},{8,4},{12,8},{16,12},{20,16},{24,20},{28,24},{1,29},{... | collective-permute-start | bytes 1544 | tf_op jit(solution)/shard_map/ppermute | solution.py:22
  9.9 7.5 %collective-permute-start.4 = (s32[1,128]{1,0:T(1,128)}, s32[1,128]{1,0:T(1,128)S(1)}, u32[]{:S(2)}, u32[]{:S(2)}) collective-permute-start(s32[1,128]{1,0:T(1,128)} %bitcast.196), channel_id=1, source_target_pairs={{0,4},{4,8},{8,12},{12,16},{16,20},{20,24},{24,28},{28,0},{1,5},{5... | collective-permute-start | bytes 1544 | tf_op jit(solution)/shard_map/ppermute | solution.py:22
  9.9 10.2 %collective-permute-start = (s32[1,128]{1,0:T(1,128)}, s32[1,128]{1,0:T(1,128)S(1)}, u32[]{:S(2)}, u32[]{:S(2)}) collective-permute-start(s32[1,128]{1,0:T(1,128)} %bitcast.189), channel_id=1, source_target_pairs={{0,28},{4,0},{8,4},{12,8},{16,12},{20,16},{24,20},{28,24},{1,29},{... | collective-permute-start | bytes 1544 | tf_op jit(solution)/shard_map/ppermute | solution.py:22
  12.5 7.6 %collective-permute-start.3 = (s32[1,128]{1,0:T(1,128)}, s32[1,128]{1,0:T(1,128)S(1)}, u32[]{:S(2)}, u32[]{:S(2)}) collective-permute-start(s32[1,128]{1,0:T(1,128)} %bitcast.190), channel_id=1, source_target_pairs={{0,4},{4,8},{8,12},{12,16},{16,20},{20,24},{24,28},{28,0},{1,5},{5... | collective-permute-start | bytes 1544 | tf_op jit(solution)/shard_map/ppermute | solution.py:22
  12.5 51.2 %collective-permute-start.2 = (bf16[1,128,128]{2,1,0:T(8,128)(2,1)}, bf16[1,128,128]{2,1,0:T(8,128)(2,1)}, u32[]{:S(2)}, u32[]{:S(2)}) collective-permute-start(bf16[1,128,128]{2,1,0:T(8,128)(2,1)} %bitcast.187), channel_id=1, source_target_pairs={{0,28},{4,0},{8,4},{12,8},{16,12},{20,16},{24,20},{28,24},{1,29},{... | collective-permute-start | bytes 98312 | tf_op jit(solution)/shard_map/ppermute | solution.py:22
  17.3 47.5 %collective-permute-start.5 = (bf16[1,128,128]{2,1,0:T(8,128)(2,1)}, bf16[1,128,128]{2,1,0:T(8,128)(2,1)}, u32[]{:S(2)}, u32[]{:S(2)}) collective-permute-start(bf16[1,128,128]{2,1,0:T(8,128)(2,1)} %bitcast.188), channel_id=1, source_target_pairs={{0,4},{4,8},{8,12},{12,16},{16,20},{20,24},{24,28},{28,0},{1,5},{5... | collective-permute-start | bytes 98312 | tf_op jit(solution)/shard_map/ppermute | solution.py:22
  17.4 4.8 %collective-permute-start.7 = (s32[1,128]{1,0:T(1,128)S(1)}, s32[1,128]{1,0:T(1,128)S(1)}, u32[]{:S(2)}, u32[]{:S(2)}) collective-permute-start(s32[1,128]{1,0:T(1,128)S(1)} %collective-permute-done.1), channel_id=1, source_target_pairs={{0,28},{4,0},{8,4},{12,8},{16,12},{20,16},{24,20},{28,24},{1,29},{... | collective-permute-start | bytes 1544 | tf_op jit(solution)/shard_map/ppermute | solution.py:22
  20.1 1.4 collective-permute-start.6
  69.6 30.5 %collective-permute-start.8 = (bf16[1,128,128]{2,1,0:T(8,128)(2,1)}, bf16[1,128,128]{2,1,0:T(8,128)(2,1)S(1)}, u32[]{:S(2)}, u32[]{:S(2)}) collective-permute-start(bf16[1,128,128]{2,1,0:T(8,128)(2,1)} %collective-permute-done.2), channel_id=1, source_target_pairs={{0,28},{4,0},{8,4},{12,8},{16,12},{20,16},{24,20},{28,24},{1,29},{... | collective-permute-start | bytes 98312 | tf_op jit(solution)/shard_map/ppermute | solution.py:22
  109.1 7.4 %copy-start.3 = (bf16[864,128]{1,0:T(8,128)(2,1)S(1)}, bf16[864,128]{1,0:T(8,128)(2,1)}, u32[]{:S(2)}) copy-start(bf16[864,128]{1,0:T(8,128)(2,1)} %gather_fusion) | copy-start | bytes 663556
  109.1 7.4 %copy-start.4 = (bf16[864,128]{1,0:T(8,128)(2,1)S(1)}, bf16[864,128]{1,0:T(8,128)(2,1)}, u32[]{:S(2)}) copy-start(bf16[864,128]{1,0:T(8,128)(2,1)} %gather_fusion.1) | copy-start | bytes 663556
  118.1 2.2 slice-start.6
  118.1 2.8 %slice-start.7 = ((s8[6193152]{0:T(1024)(128)(4,1)}), s8[1998848]{0:T(1024)(128)(4,1)S(1)}, s32[]{:S(2)}) async-start(s8[6193152]{0:T(1024)(128)(4,1)} %bitcast.184), calls=%async_computation.9 | async-start | bytes 3997696
  120.9 1.0 copy-start.2
  121.5 3.0 %slice-start.4 = ((s8[6193152]{0:T(1024)(128)(4,1)}), s8[4194304]{0:T(1024)(128)(4,1)S(1)}, s32[]{:S(2)}) async-start(s8[6193152]{0:T(1024)(128)(4,1)} %bitcast.181), calls=%async_computation.6 | async-start | bytes 8388608
  121.9 2.9 %slice-start.5 = ((s8[6193152]{0:T(1024)(128)(4,1)}), s8[1998848]{0:T(1024)(128)(4,1)S(1)}, s32[]{:S(2)}) async-start(s8[6193152]{0:T(1024)(128)(4,1)} %bitcast.181), calls=%async_computation.7 | async-start | bytes 3997696
  124.8 3.2 %copy-start.1 = (bf16[864,256]{1,0:T(8,128)(2,1)S(1)}, bf16[864,256]{1,0:T(8,128)(2,1)}, u32[]{:S(2)}) copy-start(bf16[864,256]{1,0:T(8,128)(2,1)} %gather_fusion.5) | copy-start | bytes 1327108
  128.1 2.6 slice-start.2
  128.1 3.2 %slice-start.3 = ((s8[6193152]{0:T(1024)(128)(4,1)}), s8[1998848]{0:T(1024)(128)(4,1)S(1)}, s32[]{:S(2)}) async-start(s8[6193152]{0:T(1024)(128)(4,1)} %bitcast.178), calls=%async_computation.5 | async-start | bytes 3997696
  131.3 3.3 %copy-start = (bf16[864,256]{1,0:T(8,128)(2,1)S(1)}, bf16[864,256]{1,0:T(8,128)(2,1)}, u32[]{:S(2)}) copy-start(bf16[864,256]{1,0:T(8,128)(2,1)} %gather_fusion.2) | copy-start | bytes 1327108
  134.5 2.4 slice-start
  134.5 3.0 %slice-start.1 = ((s8[6193152]{0:T(1024)(128)(4,1)}), s8[1998848]{0:T(1024)(128)(4,1)S(1)}, s32[]{:S(2)}) async-start(s8[6193152]{0:T(1024)(128)(4,1)} %bitcast.175), calls=%async_computation.3 | async-start | bytes 3997696
Sparse Core Ops, SparseCore 0:
  150.7 108.5 reduce-scatter.1
where the time goes:
time: 270 us; the launch traced here: 269 us
  waiting for transfers between devices  110 us (41%)
  local copies, waits for them, and re-layouts  68.3 us (25%)
  other arithmetic  34.7 us (13%)
  matrix products  27.1 us (10%)
  between operations  14.4 us (5%)
  starting transfers between devices  14.2 us (5%)
    reduce_scatter x1, waiting for transfers between devices, local(): lax.psum_scatter(running[None], 'walk', scatter_dimension=2, tiled=True)  109 us
    reshape x4, local copies, waits for them, and re-layouts, green_product(): return (table * (1.0 / V)).reshape(2, row_count, col_count)  29.2 us
    dot_general x8, matrix products, green_product(): lax.dot_general(left_side, right_side, (((1,), (1,)), ((), ())), preferre...  23.8 us
    gather x4, local copies, waits for them, and re-layouts, walker_term(): jnp.take(right_side, shifted, axis=0)  15.3 us
    ppermute x9, starting transfers between devices, from_behind(): return lax.ppermute(value, axis, pairs)  14.2 us
    another operation x4, other arithmetic, walker_term(): return jnp.stack([real_term, imag_term])  10.4 us
    gather x4, local copies, waits for them, and re-layouts, walker_term(): jnp.take(imag_part, shifted, axis=0)  10.2 us
    gather x4, local copies, waits for them, and re-layouts, walker_term(): jnp.take(real_part, shifted, axis=0)  10.2 us
  transfers between devices with their start and end apart: 10, of which 2 were waited for; matrix products, arithmetic and copies ran while one was open for 27% of the time, Pallas kernels for 0%

commit v1 on v0

v1 whole, which is shorter than its diff:
```python
import functools
import math

import jax
import jax.numpy as jnp
from jax import lax
from jax.experimental import pallas as pl
from jax.experimental.pallas import tpu as pltpu
from jax.sharding import PartitionSpec as P

SIDE = 6
TGRID = 1024
OFFSETS = (0, 1, -1, 2)


def sine(units):
    wrapped = ((units + 1024) & 2047) - 1024
    folded = jnp.where(wrapped > 512, 1024 - wrapped, wrapped)
    folded = jnp.where(wrapped < -512, -1024 - wrapped, folded)
    x = folded.astype(jnp.float32) * (math.pi / 1024.0)
    y = x * x
    total = jnp.full_like(y, 1.0 / math.factorial(13))
    for order in (11, 9, 7, 5, 3, 1):
        sign = -1.0 if (order // 2) % 2 else 1.0
        total = total * y + sign / math.factorial(order)
    return total * x


def sixth_turn(m):
    r = m - 6 * ((m * 10923) >> 16)
    half = jnp.where((r == 1) | (r == 5), 0.5, -0.5)
    cosine = jnp.where(r == 0, 1.0, jnp.where(r == 3, -1.0, half))
    root = math.sqrt(3.0) / 2.0
    side = jnp.where(r < 3, root, -root)
    return cosine.astype(jnp.float32), jnp.where((r == 0) | (r == 3), 0.0, side).astype(jnp.float32)


def kernel(
    walkers, m_ref, tl_ref, freq_ref, q_ref, out_ref,
    odd, turn_c, turn_s, both, table, moved, left_a, left_b, left_c, right_b,
):
    nf = freq_ref.shape[0]
    v = m_ref.shape[-1]
    nk = SIDE * SIDE
    own_k = out_ref.shape[2] // nf
    cols = out_ref.shape[3]
    first_k = lax.axis_index("walk") * own_k

    row = lax.broadcasted_iota(jnp.int32, (nf, v), 0)
    freq = jnp.zeros((nf, v), jnp.int32)
    for f in range(nf):
        freq = jnp.where(row == f, 2 * freq_ref[f] + 1, freq)
    odd[...] = freq
    both[...] = jnp.zeros_like(both)
    out_ref[...] = jnp.zeros_like(out_ref)
    q = q_ref[0]
    qx = (q * 43) >> 8
    qy = q - SIDE * qx

    def step(i, carry):
        matrix = m_ref[i]
        both[0:v, 0:v] = matrix
        both[v : 2 * v, v : 2 * v] = matrix
        times = tl_ref[i, 0:1]
        labels = tl_ref[i, 1:2]
        sx = (labels * 43) >> 8
        sy = labels - SIDE * sx
        k = lax.broadcasted_iota(jnp.int32, turn_c.shape, 0)
        kx = (k * 43) >> 8
        ky = k - SIDE * kx
        cosines, sines = sixth_turn(kx * sx + ky * sy)
        turn_c[...] = cosines
        turn_s[...] = sines
        cq, sq = sixth_turn(qx * sx + qy * sy)

        units = (odd[...] * times) & 2047
        ca = sine(units + 512)
        sa = sine(units)
        ca_q = ca * cq + sa * sq
        sa_q = sa * cq - ca * sq

        def turned(c, s, k):
            cb = turn_c[pl.ds(k, 1)]
            sb = turn_s[pl.ds(k, 1)]
            return c * cb + s * sb, s * cb - c * sb

        def put(ref, place, first, second, lanes):
            rows = slice(2 * nf * place, 2 * nf * (place + 1))
            ref[rows, lanes] = jnp.concatenate([first, second], axis=0).astype(jnp.bfloat16)

        low, high = slice(0, v), slice(v, 2 * v)
        for pair in range(nk // 2):
            c0, s0 = turned(ca, sa, 2 * pair)
            c1, s1 = turned(ca, sa, 2 * pair + 1)
            put(table, pair, c0, c1, low)
            put(table, pair, s0, s1, high)
            c0, s0 = turned(ca_q, sa_q, 2 * pair)
            c1, s1 = turned(ca_q, sa_q, 2 * pair + 1)
            put(moved, pair, c0, c1, low)
            put(moved, pair, s0, s1, high)
        for j in range(own_k):
            c, s = turned(ca, sa, first_k + j)
            put(left_b, j, c, -s, low)
            put(left_b, j, s, c, high)
            c, s = turned(ca_q, sa_q, first_k + j)
            put(left_c, j, c, s, low)
            put(left_c, j, s, -c, high)

        right_b[...] = jnp.dot(
            table[...], both[...], preferred_element_type=jnp.float32
        ).astype(jnp.bfloat16)
        left_a[...] = jnp.dot(
            left_c[...], both[...], preferred_element_type=jnp.float32
        ).astype(jnp.bfloat16)

        contract = (((1,), (1,)), ((), ()))
        for start in range(0, cols, 256):
            stop = min(start + 256, cols)
            shifted = lax.dot_general(
                left_a[...], moved[start:stop], contract, preferred_element_type=jnp.float32
            )
            flipped = lax.dot_general(
                left_b[...], right_b[start:stop], contract, preferred_element_type=jnp.float32
            )
            for j in range(own_k):
                re = slice(2 * nf * j, 2 * nf * j + nf)
                im = slice(2 * nf * j + nf, 2 * nf * (j + 1))
                rows = slice(nf * j, nf * (j + 1))
                out_ref[0, 0, rows, start:stop] += (
                    shifted[re] * flipped[re] - shifted[im] * flipped[im]
                )
                out_ref[0, 1, rows, start:stop] += (
                    shifted[re] * flipped[im] + shifted[im] * flipped[re]
                )
        return carry

    lax.fori_loop(0, walkers, step, 0)
    scale = 1.0 / (v * v * walkers)
    out_ref[...] = out_ref[...] * scale


def local(walker_m, vertex_times, vertex_labels, freq_index, q_index):
    groups = lax.axis_size("walk")
    owners = lax.axis_size("blk")
    v = walker_m.shape[-1]
    nf = freq_index.shape[0]
    k = SIDE * SIDE * nf
    own = k // groups
    tl = jnp.concatenate([vertex_times[0], vertex_labels[0]], axis=0)
    m = lax.all_gather(walker_m[0, 0], "walk")
    tl = lax.all_gather(tl, "walk")
    ms, tls = [], []
    for d in OFFSETS:
        if d == 0:
            ms.append(m)
            tls.append(tl)
        else:
            pairs = [((b + d) % owners, b) for b in range(owners)]
            ms.append(lax.ppermute(m, "blk", pairs))
            tls.append(lax.ppermute(tl, "blk", pairs))
    m = jnp.concatenate(ms, axis=0)
    tl = jnp.concatenate(tls, axis=0)
    walkers = m.shape[0]
    vmem = pl.BlockSpec(memory_space=pltpu.VMEM)
    smem = pl.BlockSpec(memory_space=pltpu.SMEM)
    bf16 = jnp.bfloat16
    return pl.pallas_call(
        functools.partial(kernel, walkers),
        out_shape=jax.ShapeDtypeStruct((1, 2, own, k), jnp.float32),
        in_specs=[vmem, vmem, smem, smem],
        out_specs=vmem,
        scratch_shapes=[
            pltpu.VMEM((nf, v), jnp.int32),
            pltpu.VMEM((40, v), jnp.float32),
            pltpu.VMEM((40, v), jnp.float32),
            pltpu.VMEM((2 * v, 2 * v), bf16),
            pltpu.VMEM((k, 2 * v), bf16),
            pltpu.VMEM((k, 2 * v), bf16),
            pltpu.VMEM((2 * own, 2 * v), bf16),
            pltpu.VMEM((2 * own, 2 * v), bf16),
            pltpu.VMEM((2 * own, 2 * v), bf16),
            pltpu.VMEM((k, 2 * v), bf16),
        ],
    )(m, tl, freq_index, q_index)


def solution(mesh):
    return jax.shard_map(
        local,
        mesh=mesh,
        in_specs=(
            P("walk", "blk", None, None),
            P("walk", "blk", None),
            P("walk", "blk", None),
            P(),
            P("blk"),
        ),
        out_specs=P("blk", None, "walk", None),
        check_vma=False,
    )
```

time: 270 us -> 56.9 us (0.21)
  waiting for transfers between devices: 110 us -> 4.28 us
  local copies, waits for them, and re-layouts: 68.3 us -> 0 us
  other arithmetic: 34.7 us -> 2.14 us
  matrix products: 27.1 us -> 0 us
  blocking collectives: 0 us -> 26.5 us
  Pallas kernels: 0 us -> 18 us
  between operations: 14.4 us -> 0.67 us
  starting transfers between devices: 14.2 us -> 5.1 us
    reduce_scatter x1 -> x0, waiting for transfers between devices: 109 us -> none  [local(): lax.psum_scatter(running[None], 'walk', scatter_dimension=2, tiled=True)]
    gather x12 -> x0, local copies, waits for them, and re-layouts: 35.6 us -> none  [the longest x4 15.3 us: walker_term(): jnp.take(right_side, shifted, axis=0)]
    reshape x4 -> x0, local copies, waits for them, and re-layouts: 29.2 us -> none  [green_product(): return (table * (1.0 / V)).reshape(2, row_count, col_count)]
    dot_general x12 -> x0, matrix products: 27.1 us -> none  [the longest x8 23.8 us: green_product(): lax.dot_general(left_side, right_side, (((1,), (1,)), ((), ())), preferre...]
    all_gather x0 -> x2, blocking collectives: none -> 26.5 us  [the longest x1 15.3 us: local(): m = lax.all_gather(walker_m[0, 0], 'walk')]
    pallas_call x0 -> x1, Pallas kernels: none -> 18 us  [local(): pl.pallas_call(functools.partial(kernel, walkers), out_shape=jax.ShapeDty...]
    add x2 -> x0, other arithmetic: 10.4 us -> none  [the longest x1 9.76 us: absorb(): running + walker_term(walker[0][0], walker[1][0], walker[2][0], freq_inde...]
    another operation x4 -> x0, other arithmetic: 10.4 us -> none  [walker_term(): return jnp.stack([real_term, imag_term])]
  transfers between devices with their start and end apart: 10 -> 6, of which waited for: 2 -> 2; matrix products, arithmetic and copies ran while one was open for 27% -> 2% of each run, Pallas kernels for 0% -> 0%
where the time goes in v1:
time: 56.9 us; the launch traced here: 56.7 us
  blocking collectives  26.5 us (47%)
  Pallas kernels  18 us (32%)
  starting transfers between devices  5.1 us (9%)
  waiting for transfers between devices  4.28 us (8%)
  other arithmetic  2.14 us (4%)
  between operations  0.67 us (1%)
    pallas_call x1, Pallas kernels, local(): pl.pallas_call(functools.partial(kernel, walkers), out_shape=jax.ShapeDty...  18 us
    all_gather x1, blocking collectives, local(): m = lax.all_gather(walker_m[0, 0], 'walk')  15.3 us
    all_gather x1, blocking collectives, local(): tl = lax.all_gather(tl, 'walk')  11.3 us
    ppermute x3, starting transfers between devices, local(): ms.append(lax.ppermute(m, 'blk', pairs))  5.09 us
    ppermute x3, waiting for transfers between devices, local(): tls.append(lax.ppermute(tl, 'blk', pairs))  4.27 us
  transfers between devices with their start and end apart: 6, of which 2 were waited for; matrix products, arithmetic and copies ran while one was open for 2% of the time, Pallas kernels for 0%

profile of v1, /device:TPU:0, one launch (start us, length us, event | category | flops | bytes accessed | tf_op | source)
XLA Modules:
  0.0 56.7 jit_solution(8096693883490455496)
XLA Ops:
  0.0 15.3 %all-gather = bf16[4,1,128,128]{3,2,1,0:T(8,128)(2,1)S(1)} all-gather(bf16[1,1,128,128]{3,2,1,0:T(8,128)(2,1)} %param.5), channel_id=2, replica_groups=mesh['blk'=8,'walk'=4] {'walk'}, dimensions={0}, use_global_device_ids=true | all-gather | bytes 163840 | tf_op jit(solution)/shard_map/all_gather | solution.py:150
  15.3 2.4 %collective-permute-start.2 = (bf16[4,128,128]{2,1,0:T(8,128)(2,1)S(1)}, bf16[4,128,128]{2,1,0:T(8,128)(2,1)S(1)}, u32[]{:S(2)}, u32[]{:S(2)}) collective-permute-start(bf16[4,128,128]{2,1,0:T(8,128)(2,1)S(1)} %bitcast.5), channel_id=1, source_target_pairs={{8,0},{12,4},{16,8},{20,12},{24,16},{28,20},{0,24},{4,28},{9,1},{1... | collective-permute-start | bytes 393224 | tf_op jit(solution)/shard_map/ppermute | solution.py:159
  17.7 0.0 collective-permute-start.1
  17.7 2.6 %collective-permute-start = (bf16[4,128,128]{2,1,0:T(8,128)(2,1)S(1)}, bf16[4,128,128]{2,1,0:T(8,128)(2,1)S(1)}, u32[]{:S(2)}, u32[]{:S(2)}) collective-permute-start(bf16[4,128,128]{2,1,0:T(8,128)(2,1)S(1)} %bitcast.7), channel_id=1, source_target_pairs={{4,0},{8,4},{12,8},{16,12},{20,16},{24,20},{28,24},{0,28},{5,1},{9... | collective-permute-start | bytes 393224 | tf_op jit(solution)/shard_map/ppermute | solution.py:159
  20.4 0.7 %add_bitcast_fusion = s32[1,2,128]{2,1,0:T(2,128)S(1)} fusion(s32[1,128]{1,0:T(1,128)} %bitcast.9, s32[1,128]{1,0:T(1,128)} %bitcast.10), kind=kLoop, calls=%fused_computation.2 | loop fusion | flops 256 | bytes 2048
  21.1 11.3 %all-gather.2 = s32[4,2,128]{2,1,0:T(2,128)S(1)} all-gather(s32[1,2,128]{2,1,0:T(2,128)S(1)} %add_bitcast_fusion), channel_id=3, replica_groups=mesh['blk'=8,'walk'=4] {'walk'}, dimensions={0}, use_global_device_ids=true | all-gather | bytes 5120 | tf_op jit(solution)/shard_map/all_gather | solution.py:151
  32.3 0.0 collective-permute-start.5
  32.3 0.0 collective-permute-start.4
  32.3 3.6 %collective-permute-done.5 = s32[4,2,128]{2,1,0:T(2,128)S(1)} collective-permute-done((s32[4,2,128]{2,1,0:T(2,128)S(1)}, s32[4,2,128]{2,1,0:T(2,128)S(1)}, u32[]{:S(2)}, u32[]{:S(2)}) %collective-permute-start.5) | collective-permute-done | bytes 4128 | tf_op jit(solution)/shard_map/ppermute | solution.py:160
  35.9 0.0 collective-permute-start.3
  36.6 0.0 collective-permute-done.4
  36.6 0.7 %collective-permute-done.3 = s32[4,2,128]{2,1,0:T(2,128)S(1)} collective-permute-done((s32[4,2,128]{2,1,0:T(2,128)S(1)}, s32[4,2,128]{2,1,0:T(2,128)S(1)}, u32[]{:S(2)}, u32[]{:S(2)}) %collective-permute-start.3) | collective-permute-done | bytes 4128 | tf_op jit(solution)/shard_map/ppermute | solution.py:160
  37.3 0.6 %pad_add_fusion.tl_ref = s32[16,2,128]{2,1,0:T(2,128)} fusion(s32[4,2,128]{2,1,0:T(2,128)S(1)} %collective-permute-done.5, s32[4,2,128]{2,1,0:T(2,128)S(1)} %collective-permute-done.4, s32[4,2,128]{2,1,0:T(2,128)S(1)} %collective-permute-done.3, s32[4,2,128]{2,1,0:T(2,128)S(1)} %all-gather.2), kind=kLoop, calls=%fused_computation.1 | loop fusion | flops 12288 | bytes 32768 | tf_op jit(solution)/shard_map/concatenate | solution.py:162
  37.9 0.0 collective-permute-done.2
  37.9 0.0 collective-permute-done.1
  37.9 0.0 collective-permute-done
  37.9 0.9 %pad_maximum_fusion.m_ref = bf16[16,128,128]{2,1,0:T(8,128)(2,1)} fusion(bf16[4,128,128]{2,1,0:T(8,128)(2,1)S(1)} %collective-permute-done.2, bf16[4,128,128]{2,1,0:T(8,128)(2,1)S(1)} %collective-permute-done.1, bf16[4,128,128]{2,1,0:T(8,128)(2,1)S(1)} %collective-permute-done, bf16[4,128,128]{2,1,0:T(8,128)(2,1)S(1)} %bitcast.8), kind=kLoop, calls=%fused_computation | loop fusion | flops 786432 | bytes 1048576 | tf_op jit(solution)/shard_map/concatenate | solution.py:161
  38.7 18.0 %shard_map.55 = f32[1,2,216,864]{3,2,1,0:T(8,128)} custom-call(bf16[16,128,128]{2,1,0:T(8,128)(2,1)} %pad_maximum_fusion.m_ref, s32[16,2,128]{2,1,0:T(2,128)} %pad_add_fusion.tl_ref, s32[24]{0:T(128)} %freq_ref.1, s32[1]{0:T(128)S(6)} %copy.7.q_ref), custom_call_target="tpu_custom_call" | custom-call | tf_op jit(solution)/shard_map/pallas_call | solution.py:167
Async XLA Ops:
  15.3 22.6 %collective-permute-start.2 = (bf16[4,128,128]{2,1,0:T(8,128)(2,1)S(1)}, bf16[4,128,128]{2,1,0:T(8,128)(2,1)S(1)}, u32[]{:S(2)}, u32[]{:S(2)}) collective-permute-start(bf16[4,128,128]{2,1,0:T(8,128)(2,1)S(1)} %bitcast.5), channel_id=1, source_target_pairs={{8,0},{12,4},{16,8},{20,12},{24,16},{28,20},{0,24},{4,28},{9,1},{1... | collective-permute-start | bytes 393224 | tf_op jit(solution)/shard_map/ppermute | solution.py:159
  17.7 20.1 %collective-permute-start.1 = (bf16[4,128,128]{2,1,0:T(8,128)(2,1)S(1)}, bf16[4,128,128]{2,1,0:T(8,128)(2,1)S(1)}, u32[]{:S(2)}, u32[]{:S(2)}) collective-permute-start(bf16[4,128,128]{2,1,0:T(8,128)(2,1)S(1)} %bitcast.6), channel_id=1, source_target_pairs={{28,0},{0,4},{4,8},{8,12},{12,16},{16,20},{20,24},{24,28},{29,1},{... | collective-permute-start | bytes 393224 | tf_op jit(solution)/shard_map/ppermute | solution.py:159
  17.7 20.1 %collective-permute-start = (bf16[4,128,128]{2,1,0:T(8,128)(2,1)S(1)}, bf16[4,128,128]{2,1,0:T(8,128)(2,1)S(1)}, u32[]{:S(2)}, u32[]{:S(2)}) collective-permute-start(bf16[4,128,128]{2,1,0:T(8,128)(2,1)S(1)} %bitcast.7), channel_id=1, source_target_pairs={{4,0},{8,4},{12,8},{16,12},{20,16},{24,20},{28,24},{0,28},{5,1},{9... | collective-permute-start | bytes 393224 | tf_op jit(solution)/shard_map/ppermute | solution.py:159
  32.3 3.6 %collective-permute-start.5 = (s32[4,2,128]{2,1,0:T(2,128)S(1)}, s32[4,2,128]{2,1,0:T(2,128)S(1)}, u32[]{:S(2)}, u32[]{:S(2)}) collective-permute-start(s32[4,2,128]{2,1,0:T(2,128)S(1)} %all-gather.2), channel_id=1, source_target_pairs={{8,0},{12,4},{16,8},{20,12},{24,16},{28,20},{0,24},{4,28},{9,1},{1... | collective-permute-start | bytes 12296 | tf_op jit(solution)/shard_map/ppermute | solution.py:160
  32.3 4.3 %collective-permute-start.4 = (s32[4,2,128]{2,1,0:T(2,128)S(1)}, s32[4,2,128]{2,1,0:T(2,128)S(1)}, u32[]{:S(2)}, u32[]{:S(2)}) collective-permute-start(s32[4,2,128]{2,1,0:T(2,128)S(1)} %all-gather.2), channel_id=1, source_target_pairs={{28,0},{0,4},{4,8},{8,12},{12,16},{16,20},{20,24},{24,28},{29,1},{... | collective-permute-start | bytes 12296 | tf_op jit(solution)/shard_map/ppermute | solution.py:160
  35.9 1.3 %collective-permute-start.3 = (s32[4,2,128]{2,1,0:T(2,128)S(1)}, s32[4,2,128]{2,1,0:T(2,128)S(1)}, u32[]{:S(2)}, u32[]{:S(2)}) collective-permute-start(s32[4,2,128]{2,1,0:T(2,128)S(1)} %all-gather.2), channel_id=1, source_target_pairs={{4,0},{8,4},{12,8},{16,12},{20,16},{24,20},{28,24},{0,28},{5,1},{9... | collective-permute-start | bytes 12296 | tf_op jit(solution)/shard_map/ppermute | solution.py:160

commit v2 on v1

--- a/solution.py
+++ b/solution.py
@@ -11,6 +11,7 @@
 SIDE = 6
 TGRID = 1024
 OFFSETS = (0, 1, -1, 2)
+FORWARD = (2, 2, 3)
 
 
 def sine(units):
@@ -35,16 +36,79 @@
     return cosine.astype(jnp.float32), jnp.where((r == 0) | (r == 3), 0.0, side).astype(jnp.float32)
 
 
+def visits(groups):
+    around = sorted(range(1, groups), key=lambda z: min(z, groups - z))
+    near = [(0, d) for d in range(len(OFFSETS))]
+    far = [(z, 0) for z in around]
+    return near + far + [(z, d) for z in around for d in range(1, len(OFFSETS))]
+
+
 def kernel(
-    walkers, m_ref, tl_ref, freq_ref, q_ref, out_ref,
+    groups, owners, m_in, t_in, l_in, freq_ref, q_ref, out_ref,
+    m_ref, t_ref, l_ref, send_sem, recv_sem,
     odd, turn_c, turn_s, both, table, moved, left_a, left_b, left_c, right_b,
 ):
+    order = visits(groups)
+    walkers = len(order)
+    w = lax.axis_index("walk")
+    b = lax.axis_index("blk")
+
+    def to_walk(z):
+        return {"walk": lax.rem(w + groups - z, groups)}
+
+    def to_blk(d):
+        return {"blk": lax.rem(b + owners - OFFSETS[d], owners)}
+
+    def copies(sources, slot, device):
+        return [
+            pltpu.make_async_remote_copy(
+                src_ref=source,
+                dst_ref=held.at[slot],
+                send_sem=send_sem.at[kind, slot],
+                recv_sem=recv_sem.at[kind, slot],
+                device_id=device,
+                device_id_type=pl.DeviceIdType.MESH,
+            )
+            for kind, (source, held) in enumerate(zip(sources, (m_ref, t_ref, l_ref)))
+        ]
+
+    own = (m_in.at[0, 0], t_in.at[0], l_in.at[0])
+
+    def held_at(slot):
+        return (m_ref.at[slot], t_ref.at[slot], l_ref.at[slot])
+
+    def arrived(slot):
+        for copy in copies(held_at(slot), slot, to_walk(1)):
+            copy.wait_recv()
+
+    barrier = pltpu.get_barrier_semaphore()
+    peers = [{"walk": lax.rem(w + z, groups)} for z in range(1, groups)]
+    reach = sorted({d % owners for d in OFFSETS + tuple(-d for d in OFFSETS)} - {0})
+    peers += [{"blk": lax.rem(b + d, owners)} for d in reach]
+    for peer in peers:
+        pl.semaphore_signal(barrier, inc=1, device_id=peer, device_id_type=pl.DeviceIdType.MESH)
+    pl.semaphore_wait(barrier, len(peers))
+    for z, d in [o for o in order if o[0] and not o[1]] + [o for o in order if o[1] and not o[0]]:
+        for copy in copies(own, order.index((z, d)), to_walk(z) if z else to_blk(d)):
+            copy.start()
+
+    def forward(z):
+        slot = order.index((z, 0))
+        arrived(slot)
+        for d in range(1, len(OFFSETS)):
+            for copy in copies(held_at(slot), order.index((z, d)), to_blk(d)):
+                copy.start()
+
+    m_ref[0] = m_in[0, 0]
+    t_ref[0] = t_in[0]
+    l_ref[0] = l_in[0]
+
     nf = freq_ref.shape[0]
     v = m_ref.shape[-1]
     nk = SIDE * SIDE
     own_k = out_ref.shape[2] // nf
     cols = out_ref.shape[3]
-    first_k = lax.axis_index("walk") * own_k
+    first_k = w * own_k
 
     row = lax.broadcasted_iota(jnp.int32, (nf, v), 0)
     freq = jnp.zeros((nf, v), jnp.int32)
@@ -58,11 +122,23 @@
     qy = q - SIDE * qx
 
     def step(i, carry):
+        for turn, z in enumerate([z for z, d in order if z and not d]):
+            @pl.when(i == FORWARD[min(turn, len(FORWARD) - 1)])
+            def _(z=z):
+                forward(z)
+
+        first_far = order.index((0, len(OFFSETS) - 1)) + 1
+        last_far = first_far + groups - 1
+
+        @pl.when(((i > 0) & (i < first_far)) | (i >= last_far))
+        def _():
+            arrived(i)
+
         matrix = m_ref[i]
         both[0:v, 0:v] = matrix
         both[v : 2 * v, v : 2 * v] = matrix
-        times = tl_ref[i, 0:1]
-        labels = tl_ref[i, 1:2]
+        times = t_ref[i]
+        labels = l_ref[i]
         sx = (labels * 43) >> 8
         sy = labels - SIDE * sx
         k = lax.broadcasted_iota(jnp.int32, turn_c.shape, 0)
@@ -137,6 +213,9 @@
     lax.fori_loop(0, walkers, step, 0)
     scale = 1.0 / (v * v * walkers)
     out_ref[...] = out_ref[...] * scale
+    for slot in range(1, walkers):
+        for copy in copies(held_at(slot), slot, to_walk(1)):
+            copy.wait_send()
 
 
 def local(walker_m, vertex_times, vertex_labels, freq_index, q_index):
@@ -146,30 +225,21 @@
     nf = freq_index.shape[0]
     k = SIDE * SIDE * nf
     own = k // groups
-    tl = jnp.concatenate([vertex_times[0], vertex_labels[0]], axis=0)
-    m = lax.all_gather(walker_m[0, 0], "walk")
-    tl = lax.all_gather(tl, "walk")
-    ms, tls = [], []
-    for d in OFFSETS:
-        if d == 0:
-            ms.append(m)
-            tls.append(tl)
-        else:
-            pairs = [((b + d) % owners, b) for b in range(owners)]
-            ms.append(lax.ppermute(m, "blk", pairs))
-            tls.append(lax.ppermute(tl, "blk", pairs))
-    m = jnp.concatenate(ms, axis=0)
-    tl = jnp.concatenate(tls, axis=0)
-    walkers = m.shape[0]
+    walkers = groups * len(OFFSETS)
     vmem = pl.BlockSpec(memory_space=pltpu.VMEM)
     smem = pl.BlockSpec(memory_space=pltpu.SMEM)
     bf16 = jnp.bfloat16
     return pl.pallas_call(
-        functools.partial(kernel, walkers),
+        functools.partial(kernel, groups, owners),
         out_shape=jax.ShapeDtypeStruct((1, 2, own, k), jnp.float32),
-        in_specs=[vmem, vmem, smem, smem],
+        in_specs=[vmem, vmem, vmem, smem, smem],
         out_specs=vmem,
         scratch_shapes=[
+            pltpu.VMEM((walkers, v, v), bf16),
+            pltpu.VMEM((walkers, 1, v), jnp.int32),
+            pltpu.VMEM((walkers, 1, v), jnp.int32),
+            pltpu.SemaphoreType.DMA((3, walkers)),
+            pltpu.SemaphoreType.DMA((3, walkers)),
             pltpu.VMEM((nf, v), jnp.int32),
             pltpu.VMEM((40, v), jnp.float32),
             pltpu.VMEM((40, v), jnp.float32),
@@ -181,7 +251,8 @@
             pltpu.VMEM((2 * own, 2 * v), bf16),
             pltpu.VMEM((k, 2 * v), bf16),
         ],
-    )(m, tl, freq_index, q_index)
+        compiler_params=pltpu.CompilerParams(collective_id=0, has_side_effects=True),
+    )(walker_m, vertex_times, vertex_labels, freq_index, q_index)
 
 
 def solution(mesh):

time: 56.9 us -> 30.6 us (0.54)
  blocking collectives: 26.5 us -> 0 us
  Pallas kernels: 18 us -> 27.1 us
  starting transfers between devices: 5.1 us -> 0 us
  waiting for transfers between devices: 4.28 us -> 0 us
  local copies, waits for them, and re-layouts: 0 us -> 2.63 us
  other arithmetic: 2.14 us -> 0 us
    all_gather x2 -> x0, blocking collectives: 26.5 us -> none  [the longest x1 15.3 us: local(): m = lax.all_gather(walker_m[0, 0], 'walk')]
    pallas_call x1, Pallas kernels: 18 us -> 27.1 us  [local(): pl.pallas_call(functools.partial(kernel, groups, owners), out_shape=jax.S...]
    ppermute x6 -> x0, starting transfers between devices: 5.1 us -> none  [the longest x3 5.09 us: local(): ms.append(lax.ppermute(m, 'blk', pairs))]
    ppermute x6 -> x0, waiting for transfers between devices: 4.28 us -> none  [the longest x3 4.27 us: local(): tls.append(lax.ppermute(tl, 'blk', pairs))]
    unnamed x0 -> x1, local copies, waits for them, and re-layouts: none -> 2.63 us
    concatenate x2 -> x0, other arithmetic: 1.46 us -> none  [the longest x1 0.86 us: local(): m = jnp.concatenate(ms, axis=0)]
    unnamed x1 -> x0, other arithmetic: 0.68 us -> none
  transfers between devices with their start and end apart: 6 -> 0, of which waited for: 2 -> 0; matrix products, arithmetic and copies ran while one was open for 2% -> 0% of each run, Pallas kernels for 0% -> 0%
where the time goes in v2:
time: 30.6 us; the launch traced here: 30.4 us
  Pallas kernels  27.1 us (89%)
  local copies, waits for them, and re-layouts  2.63 us (9%)
  between operations  0.66 us (2%)
    pallas_call x1, Pallas kernels, local(): pl.pallas_call(functools.partial(kernel, groups, owners), out_shape=jax.S...  27.1 us
    unnamed x1, local copies, waits for them, and re-layouts  2.63 us

profile of v2, /device:TPU:0, one launch (start us, length us, event | category | flops | bytes accessed | tf_op | source)
XLA Modules:
  0.0 30.4 jit_solution(7051843648763825597)
XLA Ops:
  0.7 27.1 %shard_map.55 = f32[1,2,216,864]{3,2,1,0:T(8,128)} custom-call(bf16[1,1,128,128]{3,2,1,0:T(8,128)(2,1)} %m_in.1, s32[1,1,128]{2,1,0:T(1,128)} %t_in.1, s32[1,1,128]{2,1,0:T(1,128)} %l_in.1, s32[24]{0:T(128)} %freq_ref.1, s32[1]{0:T(128)S(6)} %copy.7.q_ref), custom_call_target="tpu_custom_call" | custom-call | tf_op jit(solution)/shard_map/pallas_call | solution.py:232
  27.8 2.6 %copy.8 = f32[1,2,216,864]{3,2,1,0:T(8,128)} copy(f32[1,2,216,864]{3,2,1,0:T(8,128)} %shard_map.55) | data formatting | bytes 2985984

commit v3 on v2

--- a/solution.py
+++ b/solution.py
@@ -46,7 +46,7 @@
 def kernel(
     groups, owners, m_in, t_in, l_in, freq_ref, q_ref, out_ref,
     m_ref, t_ref, l_ref, send_sem, recv_sem,
-    odd, turn_c, turn_s, both, table, moved, left_a, left_b, left_c, right_b,
+    odd, turn_c, turn_s, both, table, left_c, *buffers,
 ):
     order = visits(groups)
     walkers = len(order)
@@ -87,11 +87,6 @@
     peers += [{"blk": lax.rem(b + d, owners)} for d in reach]
     for peer in peers:
         pl.semaphore_signal(barrier, inc=1, device_id=peer, device_id_type=pl.DeviceIdType.MESH)
-    pl.semaphore_wait(barrier, len(peers))
-    for z, d in [o for o in order if o[0] and not o[1]] + [o for o in order if o[1] and not o[0]]:
-        for copy in copies(own, order.index((z, d)), to_walk(z) if z else to_blk(d)):
-            copy.start()
-
     def forward(z):
         slot = order.index((z, 0))
         arrived(slot)
@@ -121,7 +116,7 @@
     qx = (q * 43) >> 8
     qy = q - SIDE * qx
 
-    def step(i, carry):
+    def before(i):
         for turn, z in enumerate([z for z, d in order if z and not d]):
             @pl.when(i == FORWARD[min(turn, len(FORWARD) - 1)])
             def _(z=z):
@@ -130,10 +125,11 @@
         first_far = order.index((0, len(OFFSETS) - 1)) + 1
         last_far = first_far + groups - 1
 
-        @pl.when(((i > 0) & (i < first_far)) | (i >= last_far))
+        @pl.when((i < first_far) | (i >= last_far))
         def _():
             arrived(i)
 
+    def prepare(i, moved, left_a, left_b, right_b):
         matrix = m_ref[i]
         both[0:v, 0:v] = matrix
         both[v : 2 * v, v : 2 * v] = matrix
@@ -182,13 +178,14 @@
             put(left_c, j, c, s, low)
             put(left_c, j, s, -c, high)
 
+        scale = 1.0 / (v * v * walkers)
         right_b[...] = jnp.dot(
             table[...], both[...], preferred_element_type=jnp.float32
         ).astype(jnp.bfloat16)
-        left_a[...] = jnp.dot(
-            left_c[...], both[...], preferred_element_type=jnp.float32
-        ).astype(jnp.bfloat16)
-
+        product = jnp.dot(left_c[...], both[...], preferred_element_type=jnp.float32)
+        left_a[...] = (product.astype(jnp.bfloat16).astype(jnp.float32) * scale).astype(jnp.bfloat16)
+
+    def absorb(moved, left_a, left_b, right_b):
         contract = (((1,), (1,)), ((), ()))
         for start in range(0, cols, 256):
             stop = min(start + 256, cols)
@@ -208,11 +205,28 @@
                 out_ref[0, 1, rows, start:stop] += (
                     shifted[re] * flipped[im] + shifted[im] * flipped[re]
                 )
+
+    first, second = buffers[: len(buffers) // 2], buffers[len(buffers) // 2 :]
+    prepare(0, *first)
+    absorb(*first)
+    pl.semaphore_wait(barrier, len(peers))
+    for z, d in [o for o in order if o[0] and not o[1]] + [o for o in order if o[1] and not o[0]]:
+        for copy in copies(own, order.index((z, d)), to_walk(z) if z else to_blk(d)):
+            copy.start()
+
+    before(1)
+    prepare(1, *first)
+
+    def step(turn, carry):
+        i = 1 + 2 * turn
+        for n, now, later in ((1, first, second), (2, second, first)):
+            before(i + n)
+            absorb(*now)
+            prepare(i + n, *later)
         return carry
 
-    lax.fori_loop(0, walkers, step, 0)
-    scale = 1.0 / (v * v * walkers)
-    out_ref[...] = out_ref[...] * scale
+    lax.fori_loop(0, (walkers - 2) // 2, step, 0)
+    absorb(*first)
     for slot in range(1, walkers):
         for copy in copies(held_at(slot), slot, to_walk(1)):
             copy.wait_send()
@@ -231,7 +245,7 @@
     bf16 = jnp.bfloat16
     return pl.pallas_call(
         functools.partial(kernel, groups, owners),
-        out_shape=jax.ShapeDtypeStruct((1, 2, own, k), jnp.float32),
+        out_shape=pltpu.VMEM((1, 2, own, k), jnp.float32),
         in_specs=[vmem, vmem, vmem, smem, smem],
         out_specs=vmem,
         scratch_shapes=[
@@ -245,8 +259,11 @@
             pltpu.VMEM((40, v), jnp.float32),
             pltpu.VMEM((2 * v, 2 * v), bf16),
             pltpu.VMEM((k, 2 * v), bf16),
+            pltpu.VMEM((2 * own, 2 * v), bf16),
+        ]
+        + 2
+        * [
             pltpu.VMEM((k, 2 * v), bf16),
-            pltpu.VMEM((2 * own, 2 * v), bf16),
             pltpu.VMEM((2 * own, 2 * v), bf16),
             pltpu.VMEM((2 * own, 2 * v), bf16),
             pltpu.VMEM((k, 2 * v), bf16),

time: 30.6 us -> 30.4 us (level)
  local copies, waits for them, and re-layouts: 2.63 us -> 1.14 us
  Pallas kernels: 27.1 us -> 28.4 us
    unnamed x1, local copies, waits for them, and re-layouts: 2.63 us -> 1.14 us
    pallas_call x1, Pallas kernels: 27.1 us -> 28.4 us  [local(): pl.pallas_call(functools.partial(kernel, groups, owners), out_shape=pltpu...]
where the time goes in v3:
time: 30.4 us; the launch traced here: 30.2 us
  Pallas kernels  28.4 us (93%)
  local copies, waits for them, and re-layouts  1.14 us (4%)
  between operations  0.66 us (2%)
    pallas_call x1, Pallas kernels, local(): pl.pallas_call(functools.partial(kernel, groups, owners), out_shape=pltpu...  28.4 us
    unnamed x1, local copies, waits for them, and re-layouts  1.14 us

profile of v3, /device:TPU:0, one launch (start us, length us, event | category | flops | bytes accessed | tf_op | source)
XLA Modules:
  0.0 30.2 jit_solution(1550998035478244901)
XLA Ops:
  0.7 28.4 %shard_map.55 = f32[1,2,216,864]{3,2,1,0:T(8,128)S(1)} custom-call(bf16[1,1,128,128]{3,2,1,0:T(8,128)(2,1)} %m_in.1, s32[1,1,128]{2,1,0:T(1,128)} %t_in.1, s32[1,1,128]{2,1,0:T(1,128)} %l_in.1, s32[24]{0:T(128)} %freq_ref.1, s32[1]{0:T(128)S(6)} %copy.8.q_ref), custom_call_target="tpu_custom_call" | custom-call | tf_op jit(solution)/shard_map/pallas_call | solution.py:246
  29.1 1.1 %copy.7 = f32[1,2,216,864]{3,2,1,0:T(8,128)} copy(f32[1,2,216,864]{3,2,1,0:T(8,128)S(1)} %shard_map.55) | data formatting | bytes 2985984

commit v4 on v2

--- a/solution.py
+++ b/solution.py
@@ -11,7 +11,7 @@
 SIDE = 6
 TGRID = 1024
 OFFSETS = (0, 1, -1, 2)
-FORWARD = (2, 2, 3)
+FORWARD = (2, 3, 4)
 
 
 def sine(units):
@@ -87,6 +87,11 @@
     peers += [{"blk": lax.rem(b + d, owners)} for d in reach]
     for peer in peers:
         pl.semaphore_signal(barrier, inc=1, device_id=peer, device_id_type=pl.DeviceIdType.MESH)
+    m_ref[0] = m_in[0, 0]
+    t_ref[0] = t_in[0]
+    l_ref[0] = l_in[0]
+    both[...] = jnp.zeros_like(both)
+    out_ref[...] = jnp.zeros_like(out_ref)
     pl.semaphore_wait(barrier, len(peers))
     for z, d in [o for o in order if o[0] and not o[1]] + [o for o in order if o[1] and not o[0]]:
         for copy in copies(own, order.index((z, d)), to_walk(z) if z else to_blk(d)):
@@ -99,9 +104,6 @@
             for copy in copies(held_at(slot), order.index((z, d)), to_blk(d)):
                 copy.start()
 
-    m_ref[0] = m_in[0, 0]
-    t_ref[0] = t_in[0]
-    l_ref[0] = l_in[0]
 
     nf = freq_ref.shape[0]
     v = m_ref.shape[-1]
@@ -115,22 +117,24 @@
     for f in range(nf):
         freq = jnp.where(row == f, 2 * freq_ref[f] + 1, freq)
     odd[...] = freq
-    both[...] = jnp.zeros_like(both)
-    out_ref[...] = jnp.zeros_like(out_ref)
     q = q_ref[0]
     qx = (q * 43) >> 8
     qy = q - SIDE * qx
 
-    def step(i, carry):
+    scale = 1.0 / (v * v * walkers)
+
+    def step(visit, carry):
+        swap = (lax.rem(b, 2) == 1) & ((visit == 1) | (visit == 2))
+        i = jnp.where(swap, 3 - visit, visit)
         for turn, z in enumerate([z for z, d in order if z and not d]):
-            @pl.when(i == FORWARD[min(turn, len(FORWARD) - 1)])
+            @pl.when(visit == FORWARD[min(turn, len(FORWARD) - 1)])
             def _(z=z):
                 forward(z)
 
         first_far = order.index((0, len(OFFSETS) - 1)) + 1
         last_far = first_far + groups - 1
 
-        @pl.when(((i > 0) & (i < first_far)) | (i >= last_far))
+        @pl.when(((visit > 0) & (visit < first_far)) | (visit >= last_far))
         def _():
             arrived(i)
 
@@ -185,9 +189,8 @@
         right_b[...] = jnp.dot(
             table[...], both[...], preferred_element_type=jnp.float32
         ).astype(jnp.bfloat16)
-        left_a[...] = jnp.dot(
-            left_c[...], both[...], preferred_element_type=jnp.float32
-        ).astype(jnp.bfloat16)
+        product = jnp.dot(left_c[...], both[...], preferred_element_type=jnp.float32)
+        left_a[...] = (product.astype(jnp.bfloat16).astype(jnp.float32) * scale).astype(jnp.bfloat16)
 
         contract = (((1,), (1,)), ((), ()))
         for start in range(0, cols, 256):
@@ -211,8 +214,6 @@
         return carry
 
     lax.fori_loop(0, walkers, step, 0)
-    scale = 1.0 / (v * v * walkers)
-    out_ref[...] = out_ref[...] * scale
     for slot in range(1, walkers):
         for copy in copies(held_at(slot), slot, to_walk(1)):
             copy.wait_send()
@@ -231,7 +232,7 @@
     bf16 = jnp.bfloat16
     return pl.pallas_call(
         functools.partial(kernel, groups, owners),
-        out_shape=jax.ShapeDtypeStruct((1, 2, own, k), jnp.float32),
+        out_shape=pltpu.VMEM((1, 2, own, k), jnp.float32),
         in_specs=[vmem, vmem, vmem, smem, smem],
         out_specs=vmem,
         scratch_shapes=[

time: 30.6 us -> 27.3 us (0.89)
  Pallas kernels: 27.1 us -> 25.3 us
  local copies, waits for them, and re-layouts: 2.63 us -> 1.14 us
    pallas_call x1, Pallas kernels: 27.1 us -> 25.3 us  [local(): pl.pallas_call(functools.partial(kernel, groups, owners), out_shape=pltpu...]
    unnamed x1, local copies, waits for them, and re-layouts: 2.63 us -> 1.14 us
where the time goes in v4:
time: 27.3 us; the launch traced here: 27.1 us
  Pallas kernels  25.3 us (93%)
  local copies, waits for them, and re-layouts  1.14 us (4%)
  between operations  0.66 us (2%)
    pallas_call x1, Pallas kernels, local(): pl.pallas_call(functools.partial(kernel, groups, owners), out_shape=pltpu...  25.3 us
    unnamed x1, local copies, waits for them, and re-layouts  1.14 us

profile of v4, /device:TPU:0, one launch (start us, length us, event | category | flops | bytes accessed | tf_op | source)
XLA Modules:
  0.0 27.1 jit_solution(15274911547933692979)
XLA Ops:
  0.7 25.3 %shard_map.55 = f32[1,2,216,864]{3,2,1,0:T(8,128)S(1)} custom-call(bf16[1,1,128,128]{3,2,1,0:T(8,128)(2,1)} %m_in.1, s32[1,1,128]{2,1,0:T(1,128)} %t_in.1, s32[1,1,128]{2,1,0:T(1,128)} %l_in.1, s32[24]{0:T(128)} %freq_ref.1, s32[1]{0:T(128)S(6)} %copy.8.q_ref), custom_call_target="tpu_custom_call" | custom-call | tf_op jit(solution)/shard_map/pallas_call | solution.py:233
  26.0 1.1 %copy.7 = f32[1,2,216,864]{3,2,1,0:T(8,128)} copy(f32[1,2,216,864]{3,2,1,0:T(8,128)S(1)} %shard_map.55) | data formatting | bytes 2985984
